TPU v7x, 32 devices: a whole 2x2x4 slice. The times are simulated.
32 devices in a mesh: cuts: 8 (over z, y), batch: 4 (over x, core).
Axes of the slice: x: 2, y: 2, z: 4, core: 2. Of those that a mesh axis runs over, the one named last changes fastest.
Arguments:
- blocks: bfloat16 [256, 64, 128], P(('cuts', 'batch')), may hold values from -6 to 6
- environments: bfloat16 [256, 64, 128], P(('cuts', 'batch')), may hold values from -0.5 to 0.5
- layers: bfloat16 [8, 64, 128], replicated, may hold values from -0.5 to 0.5
- selectors: bfloat16 [256, 8, 128], P(('cuts', 'batch')), may hold values from -6 to 6
- classes: int32 [32, 8], P(('cuts', 'batch')), may hold values from 1 to 8
- routing: int32 [32, 8], P(('cuts', 'batch')), may hold values from 0 to 7, each once within a row
- left_edges: bfloat16 [64, 128], replicated, may hold values from -0.5 to 0.5
- right_edges: bfloat16 [64, 128], replicated, may hold values from -0.5 to 0.5
- owner_map: int32 [4096], replicated, may hold values from 0 to 4095, each once
Outputs:
- amplitudes: float32 [2, 4096], P(None, ('cuts', 'batch'))
Inputs may be any that keep to these rules, and one draw needn't show every extreme that they name: `routing`: each holder's row is a permutation of 0 to 7. `owner_map`: A permutation of the bitstrings.
All inputs are finite; a program needn't handle non-finite values.
Results may differ from a plain program's by a relative error of at most 0.009.
Values may be sent and summed in bfloat16 or wider, within the bound.
A program may use at most 64 MiB of HBM per device.

v0:
```python
import jax
import jax.numpy as jnp
from jax import lax
from jax.sharding import PartitionSpec as P


def block_form(matrix):
    half_count = matrix.shape[-1] // 2
    real_block = matrix[..., :half_count]
    imag_block = matrix[..., half_count:]
    upper_rows = jnp.concatenate([real_block, imag_block], axis=-1)
    lower_rows = jnp.concatenate([-imag_block, real_block], axis=-1)
    return jnp.concatenate([upper_rows, lower_rows], axis=-2)


def apply_phase(product, factors):
    half_count = product.shape[-1] // 2
    prod_real = product[..., :half_count]
    prod_imag = product[..., half_count:]
    fac_real = factors[..., :half_count].astype(jnp.float32)[:, None, :]
    fac_imag = factors[..., half_count:].astype(jnp.float32)[:, None, :]
    out_real = prod_real * fac_real - prod_imag * fac_imag
    out_imag = prod_real * fac_imag + prod_imag * fac_real
    return jnp.concatenate([out_real, out_imag], axis=-1)


def advance(blocks_now, factors, levels, tables):
    slot_count = blocks_now.shape[0]
    block_rows = min(32, slot_count)
    ranking = jnp.argsort(-levels, stable=True)
    blocks_now = blocks_now[ranking]
    factors = factors[ranking]
    levels = levels[ranking]
    for layer_index in range(tables.shape[0]):
        active = jnp.sum((levels > layer_index).astype(jnp.int32))
        rounds = (active + block_rows - 1) // block_rows
        layer_factors = factors[:, layer_index, :]

        def apply(round_index, current, layer_index=layer_index, layer_factors=layer_factors):
            offset = round_index * block_rows
            portion = lax.dynamic_slice_in_dim(current, offset, block_rows, 0)
            portion_levels = lax.dynamic_slice_in_dim(levels, offset, block_rows, 0)
            portion_factors = lax.dynamic_slice_in_dim(layer_factors, offset, block_rows, 0)
            product = jnp.einsum(
                "sij,jk->sik", portion, tables[layer_index], preferred_element_type=jnp.float32
            )
            updated = apply_phase(product, portion_factors).astype(jnp.bfloat16)
            portion = jnp.where((portion_levels > layer_index)[:, None, None], updated, portion)
            return lax.dynamic_update_slice_in_dim(current, portion, offset, 0)

        blocks_now = lax.fori_loop(0, rounds, apply, blocks_now)
    return (blocks_now, ranking)


def contract(worked, partners):
    slot_count, bond_width, doubled = worked.shape
    parted = worked.reshape(slot_count, bond_width, 2, bond_width)
    products = jnp.einsum("sipj,sjk->pik", parted, partners, preferred_element_type=jnp.float32)
    real_part = products[0, :, :bond_width] - products[1, :, bond_width:]
    imag_part = products[0, :, bond_width:] + products[1, :, :bond_width]
    return (real_part, imag_part)


def amplitude_table(real_part, imag_part, left_edges, right_edges, owner_map):
    highest = lax.Precision.HIGHEST
    half_count = left_edges.shape[1] // 2
    left_real = left_edges[:, :half_count].astype(jnp.float32)
    left_imag = left_edges[:, half_count:].astype(jnp.float32)
    right_real = right_edges[:, :half_count].astype(jnp.float32)
    right_imag = right_edges[:, half_count:].astype(jnp.float32)
    wave_real = jnp.dot(real_part, right_real, precision=highest) - jnp.dot(
        imag_part, right_imag, precision=highest
    )
    wave_imag = jnp.dot(real_part, right_imag, precision=highest) + jnp.dot(
        imag_part, right_real, precision=highest
    )
    amp_real = jnp.dot(left_real.T, wave_real, precision=highest) - jnp.dot(
        left_imag.T, wave_imag, precision=highest
    )
    amp_imag = jnp.dot(left_real.T, wave_imag, precision=highest) + jnp.dot(
        left_imag.T, wave_real, precision=highest
    )
    flattened = jnp.stack([amp_real.reshape(-1), amp_imag.reshape(-1)])
    return flattened[:, owner_map]


def on_device(
    blocks, environments, layers, selectors, classes, routing, left_edges, right_edges, owner_map
):
    slot_count, bond_width, doubled = blocks.shape
    cut_count = lax.axis_size("cuts")
    member = slot_count // cut_count
    tables = block_form(layers)
    levels = classes[0]
    sending = routing[0]
    worked, ranking = advance(blocks, selectors, levels, tables)
    inverse = jnp.argsort(ranking)
    outgoing = worked[inverse[sending]].reshape(cut_count, member, bond_width, doubled)
    worked = lax.all_to_all(outgoing, "cuts", split_axis=0, concat_axis=0, tiled=True).reshape(
        slot_count, bond_width, doubled
    )
    real_part, imag_part = contract(worked, environments)
    holder_count = cut_count * lax.axis_size("batch")
    normalizer = (slot_count * holder_count) ** (-0.5)
    real_part, imag_part = lax.psum((real_part, imag_part), ("cuts", "batch"))
    amp_table = (
        amplitude_table(real_part, imag_part, left_edges, right_edges, owner_map) * normalizer
    )
    per_holder = amp_table.shape[1] // holder_count
    holder = lax.axis_index("cuts") * lax.axis_size("batch") + lax.axis_index("batch")
    return lax.dynamic_slice_in_dim(amp_table, holder * per_holder, per_holder, 1)


def solution(mesh):
    placed = (
        P(("cuts", "batch"), None, None),
        P(("cuts", "batch"), None, None),
        P(),
        P(("cuts", "batch"), None, None),
        P(("cuts", "batch"), None),
        P(("cuts", "batch"), None),
        P(),
        P(),
        P(),
    )
    return jax.shard_map(
        on_device, mesh=mesh, in_specs=placed, out_specs=P(None, ("cuts", "batch")), check_vma=False
    )
```

profile of v0, /device:TPU:0, one launch (start us, length us, event | category | flops | bytes accessed | tf_op | source)
XLA Modules:
  0.0 92.2 jit_solution(10878997560112806243)
XLA Ops:
  0.0 0.7 bitcast_negate_fusion
  0.7 1.0 %sort.34 = (s32[8]{0:T(128)}, s32[8]{0:T(128)S(1)}) sort(s32[8]{0:T(128)S(1)} %bitcast_negate_fusion, s32[8]{0:T(128)S(1)} %iota.8), dimensions={0}, to_apply=%region_0.0 | sort | flops 24 | bytes 128 | tf_op jit(solution)/shard_map/jit(argsort)/sort | solution.py:30
  1.7 1.3 %gather_fusion.1 = s32[8]{0:T(128)S(1)} fusion(s32[8]{0:T(128)} %bitcast.127, s32[1024]{0:T(1024)S(1)} %pad_clamp_fusion.2), kind=kCustom, calls=%fused_computation.1 | custom fusion | bytes 96 | tf_op jit(solution)/shard_map/gather | solution.py:33
  3.0 0.8 fusion.51
  8.8 1.3 %gather_fusion.2 = bf16[8,8,128]{2,1,0:T(8,128)(2,1)S(1)} fusion(bf16[8,8,128]{2,1,0:T(8,128)(2,1)} %param.28, s32[1024]{0:T(1024)S(1)} %pad_clamp_fusion.2), kind=kCustom, calls=%fused_computation.2 | custom fusion | bytes 32800 | tf_op jit(solution)/shard_map/gather | solution.py:32
  10.1 1.1 %slice_negate_fusion = (bf16[8,64,64]{2,1,0:T(8,128)(2,1)S(1)}, bf16[8,64,64]{2,1,0:T(8,128)(2,1)S(1)}) fusion(bf16[8,64,128]{2,1,0:T(8,128)(2,1)} %param.27), kind=kLoop, calls=%fused_computation.88 | loop fusion | flops 32768 | bytes 262144 | tf_op jit(solution)/shard_map/neg | solution.py:12
  11.2 0.6 gather_fusion
  11.8 1.0 %maximum_maximum_fusion = bf16[8,128,128]{2,1,0:T(8,128)(2,1)S(1)} fusion(bf16[8,64,64]{2,1,0:T(8,128)(2,1)S(1)} %get-tuple-element.420, bf16[8,64,64]{2,1,0:T(8,128)(2,1)S(1)} %get-tuple-element.419, bf16[8,64,128]{2,1,0:T(8,128)(2,1)} %param.27), kind=kLoop, calls=%fused_computation.85 | loop fusion | flops 786432 | bytes 524288 | tf_op jit(solution)/shard_map/concatenate | solution.py:13
  12.8 0.6 while.80
  12.9 0.2 fusion.97
  13.0 0.1 slice_convert_fusion.24
  13.1 0.2 subtract_convert_fusion.16
  13.3 0.2 maximum_select_fusion.16
  13.5 0.6 while.81
  13.5 0.2 fusion.100
  13.6 0.1 slice_convert_fusion.25
  13.7 0.2 subtract_convert_fusion.17
  13.9 0.2 maximum_select_fusion.17
  14.1 0.6 while.82
  14.1 0.2 fusion.103
  14.3 0.1 slice_convert_fusion.26
  14.4 0.2 subtract_convert_fusion.18
  14.5 0.2 maximum_select_fusion.18
  15.0 1.0 %sort.35 = (s32[8]{0:T(128)}, s32[8]{0:T(128)S(1)}) sort(s32[8]{0:T(128)S(1)} %get-tuple-element.271, s32[8]{0:T(128)S(1)} %iota.9), dimensions={0}, to_apply=%region_25.26 | sort | flops 24 | bytes 128 | tf_op jit(solution)/shard_map/jit(argsort)/sort | solution.py:97
  16.0 0.6 gather_fusion.3
  16.6 1.2 %gather_fusion.4 = bf16[8,64,128]{2,1,0:T(8,128)(2,1)} fusion(bf16[8,64,128]{2,1,0:T(8,128)(2,1)S(1)} %get-tuple-element.279, s32[1024]{0:T(1024)S(1)} %pad_clamp_fusion), kind=kCustom, calls=%fused_computation.4 | custom fusion | bytes 262176 | tf_op jit(solution)/shard_map/gather | solution.py:98
  17.8 10.2 %all-to-all-start = ((bf16[8,1,64,128]{3,2,1,0:T(8,128)(2,1)}), bf16[8,1,64,128]{3,2,1,0:T(8,128)(2,1)S(1)}, u32[]{:S(2)}, u32[]{:S(2)}) async-start(bf16[8,1,64,128]{3,2,1,0:T(8,128)(2,1)} %bitcast.21), calls=%async_computation | async-start | bytes 262144 | tf_op jit(solution)/shard_map/all_to_all | solution.py:99
  28.1 7.3 %all-to-all-done = bf16[8,1,64,128]{3,2,1,0:T(8,128)(2,1)S(1)} async-done(((bf16[8,1,64,128]{3,2,1,0:T(8,128)(2,1)}), bf16[8,1,64,128]{3,2,1,0:T(8,128)(2,1)S(1)}, u32[]{:S(2)}, u32[]{:S(2)}) %all-to-all-start) | async-done | bytes 131104 | tf_op jit(solution)/shard_map/all_to_all | solution.py:99
  35.4 0.1 reshape_reshape.3
  35.5 0.2 convolution_bitcast_fusion
  35.8 0.1 fusion.29
  35.9 38.0 %all-reduce = (f32[64,64]{1,0:T(8,128)S(1)}, f32[64,64]{1,0:T(8,128)S(1)}) all-reduce(f32[64,64]{1,0:T(8,128)S(1)} %get-tuple-element.422, f32[64,64]{1,0:T(8,128)S(1)} %get-tuple-element.421), channel_id=1, replica_groups=mesh['cuts'=8,'batch'=4] {'cuts','batch'}, use_global_device_ids=true, to_apply=%region_26.27 | all-reduce | flops 8192 | bytes 65536 | tf_op jit(solution)/shard_map/psum | solution.py:105
  73.9 0.1 fusion.42
  74.1 0.2 fusion.38
  74.3 0.2 convolution_subtract_fusion.1
  74.5 0.1 convolution_add_fusion.1
  74.7 0.2 fusion.36
  74.9 0.2 fusion.34
  75.1 0.2 fusion.25
  75.4 0.1 copy.24
  75.4 0.1 stack_reshape.6
  75.5 0.2 fusion.24
  75.8 0.1 copy.25
  75.8 0.1 stack_reshape.7
  76.0 0.6 copy.26
  76.6 14.1 %gather_fusion.5 = f32[4096,2]{1,0:T(8,128)} fusion(f32[2,4096]{0,1:T(8,128)S(1)} %copy.26, s32[4096]{0:T(1024)S(1)} %fusion.31), kind=kCustom, calls=%fused_computation.5 | custom fusion | bytes 81920 | tf_op jit(solution)/shard_map/gather | solution.py:84
  90.7 0.8 fusion.28
  91.6 0.6 copy.27
  (35 shorter events, 0.2 us)
Async XLA Ops:
  0.0 11.2 %copy-start = (bf16[8,64,128]{2,1,0:T(8,128)(2,1)S(1)}, bf16[8,64,128]{2,1,0:T(8,128)(2,1)}, u32[]{:S(2)}) copy-start(bf16[8,64,128]{2,1,0:T(8,128)(2,1)} %param.25) | copy-start | bytes 393220
  14.9 1.1 %copy-start.5 = (s32[1,8]{1,0:T(1,128)S(1)}, s32[1,8]{1,0:T(1,128)}, u32[]{:S(2)}) copy-start(s32[1,8]{1,0:T(1,128)} %param.30) | copy-start | bytes 100
  14.9 13.1 %copy-start.3 = (s32[4096]{0:T(1024)S(1)}, s32[4096]{0:T(1024)}, u32[]{:S(2)}) copy-start(s32[4096]{0:T(1024)} %param.33) | copy-start | bytes 49156
  14.9 20.6 %copy-start.4 = (bf16[8,64,128]{2,1,0:T(8,128)(2,1)S(1)}, bf16[8,64,128]{2,1,0:T(8,128)(2,1)}, u32[]{:S(2)}) copy-start(bf16[8,64,128]{2,1,0:T(8,128)(2,1)} %param.26) | copy-start | bytes 393220
  15.0 59.0 %copy-start.1 = (bf16[64,128]{1,0:T(8,128)(2,1)S(1)}, bf16[64,128]{1,0:T(8,128)(2,1)}, u32[]{:S(2)}) copy-start(bf16[64,128]{1,0:T(8,128)(2,1)} %param.32) | copy-start | bytes 49156
  15.0 59.7 %copy-start.2 = (bf16[64,128]{1,0:T(8,128)(2,1)S(1)}, bf16[64,128]{1,0:T(8,128)(2,1)}, u32[]{:S(2)}) copy-start(bf16[64,128]{1,0:T(8,128)(2,1)} %param.31) | copy-start | bytes 49156
  17.8 17.6 %all-to-all-start = ((bf16[8,1,64,128]{3,2,1,0:T(8,128)(2,1)}), bf16[8,1,64,128]{3,2,1,0:T(8,128)(2,1)S(1)}, u32[]{:S(2)}, u32[]{:S(2)}) async-start(bf16[8,1,64,128]{3,2,1,0:T(8,128)(2,1)} %bitcast.21), calls=%async_computation | async-start | bytes 262144 | tf_op jit(solution)/shard_map/all_to_all | solution.py:99
where the time goes:
time: 92.8 us; the launch traced here: 92.2 us
  blocking collectives  38 us (41%)
  local copies, waits for them, and re-layouts  20.9 us (23%)
  starting transfers between devices  10.2 us (11%)
  other arithmetic  7.64 us (8%)
  waiting for transfers between devices  7.32 us (8%)
  between operations  5.54 us (6%)
  matrix products  2.34 us (3%)
    psum x1, blocking collectives, on_device(): real_part, imag_part = lax.psum((real_part, imag_part), ('cuts', 'batch'))  38 us
    gather x1, local copies, waits for them, and re-layouts, amplitude_table(): return flattened[:, owner_map]  14.1 us
    all_to_all x1, starting transfers between devices, on_device(): lax.all_to_all(outgoing, 'cuts', split_axis=0, concat_axis=0, tiled=True)  10.2 us
    all_to_all x1, waiting for transfers between devices, on_device(): lax.all_to_all(outgoing, 'cuts', split_axis=0, concat_axis=0, tiled=True)  7.32 us
  transfers between devices with their start and end apart: 1, of which 1 were waited for; matrix products, arithmetic and copies ran while one was open for 0% of the time, Pallas kernels for 0%

commit v1 on v0

--- a/solution.py
+++ b/solution.py
@@ -102,7 +102,7 @@
     real_part, imag_part = contract(worked, environments)
     holder_count = cut_count * lax.axis_size("batch")
     normalizer = (slot_count * holder_count) ** (-0.5)
-    real_part, imag_part = lax.psum((real_part, imag_part), ("cuts", "batch"))
+    real_part, imag_part = lax.psum(lax.psum((real_part, imag_part), "batch"), "cuts")
     amp_table = (
         amplitude_table(real_part, imag_part, left_edges, right_edges, owner_map) * normalizer
     )

time: 92.8 us -> 100 us (1.078)
  blocking collectives: 38 us -> 45.8 us
    psum x1 -> x2, blocking collectives: 38 us -> 45.8 us  [the longest x1 34.8 us: on_device(): lax.psum(lax.psum((real_part, imag_part), 'batch'), 'cuts')]
where the time goes in v1:
time: 100 us; the launch traced here: 99.9 us
  blocking collectives  45.8 us (46%)
  local copies, waits for them, and re-layouts  20.9 us (21%)
  starting transfers between devices  10.2 us (10%)
  other arithmetic  7.64 us (8%)
  waiting for transfers between devices  7.32 us (7%)
  between operations  5.55 us (6%)
  matrix products  2.34 us (2%)
    psum x1, blocking collectives, on_device(): lax.psum(lax.psum((real_part, imag_part), 'batch'), 'cuts')  34.8 us
    gather x1, local copies, waits for them, and re-layouts, amplitude_table(): return flattened[:, owner_map]  14.1 us
    psum x1, blocking collectives, on_device(): lax.psum((real_part, imag_part), 'batch')  11 us
    all_to_all x1, starting transfers between devices, on_device(): lax.all_to_all(outgoing, 'cuts', split_axis=0, concat_axis=0, tiled=True)  10.2 us
    all_to_all x1, waiting for transfers between devices, on_device(): lax.all_to_all(outgoing, 'cuts', split_axis=0, concat_axis=0, tiled=True)  7.32 us
  transfers between devices with their start and end apart: 1, of which 1 were waited for; matrix products, arithmetic and copies ran while one was open for 0% of the time, Pallas kernels for 0%

profile of v1, /device:TPU:0, one launch (start us, length us, event | category | flops | bytes accessed | tf_op | source)
XLA Modules:
  0.0 99.9 jit_solution(18423014781140506049)
XLA Ops:
  0.0 0.7 bitcast_negate_fusion
  0.7 1.0 sort.34
  1.7 1.3 %gather_fusion.1 = s32[8]{0:T(128)S(1)} fusion(s32[8]{0:T(128)} %bitcast.127, s32[1024]{0:T(1024)S(1)} %pad_clamp_fusion.2), kind=kCustom, calls=%fused_computation.1 | custom fusion | bytes 96 | tf_op jit(solution)/shard_map/gather | solution.py:33
  3.0 0.8 fusion.51
  8.8 1.3 %gather_fusion.2 = bf16[8,8,128]{2,1,0:T(8,128)(2,1)S(1)} fusion(bf16[8,8,128]{2,1,0:T(8,128)(2,1)} %param.28, s32[1024]{0:T(1024)S(1)} %pad_clamp_fusion.2), kind=kCustom, calls=%fused_computation.2 | custom fusion | bytes 32800 | tf_op jit(solution)/shard_map/gather | solution.py:32
  10.1 1.1 %slice_negate_fusion = (bf16[8,64,64]{2,1,0:T(8,128)(2,1)S(1)}, bf16[8,64,64]{2,1,0:T(8,128)(2,1)S(1)}) fusion(bf16[8,64,128]{2,1,0:T(8,128)(2,1)} %param.27), kind=kLoop, calls=%fused_computation.88 | loop fusion | flops 32768 | bytes 262144 | tf_op jit(solution)/shard_map/neg | solution.py:12
  11.2 0.6 gather_fusion
  11.8 1.0 %maximum_maximum_fusion = bf16[8,128,128]{2,1,0:T(8,128)(2,1)S(1)} fusion(bf16[8,64,64]{2,1,0:T(8,128)(2,1)S(1)} %get-tuple-element.422, bf16[8,64,64]{2,1,0:T(8,128)(2,1)S(1)} %get-tuple-element.421, bf16[8,64,128]{2,1,0:T(8,128)(2,1)} %param.27), kind=kLoop, calls=%fused_computation.85 | loop fusion | flops 786432 | bytes 524288 | tf_op jit(solution)/shard_map/concatenate | solution.py:13
  12.8 0.6 while.80
  12.9 0.2 fusion.97
  13.0 0.1 slice_convert_fusion.24
  13.1 0.2 subtract_convert_fusion.16
  13.3 0.2 maximum_select_fusion.16
  13.5 0.6 while.81
  13.5 0.2 fusion.100
  13.6 0.1 slice_convert_fusion.25
  13.7 0.2 subtract_convert_fusion.17
  13.9 0.2 maximum_select_fusion.17
  14.1 0.6 while.82
  14.1 0.2 fusion.103
  14.4 0.2 subtract_convert_fusion.18
  14.5 0.2 maximum_select_fusion.18
  15.0 1.0 sort.35
  16.0 0.6 gather_fusion.3
  16.6 1.2 %gather_fusion.4 = bf16[8,64,128]{2,1,0:T(8,128)(2,1)} fusion(bf16[8,64,128]{2,1,0:T(8,128)(2,1)S(1)} %get-tuple-element.279, s32[1024]{0:T(1024)S(1)} %pad_clamp_fusion), kind=kCustom, calls=%fused_computation.4 | custom fusion | bytes 262176 | tf_op jit(solution)/shard_map/gather | solution.py:98
  17.8 10.2 %all-to-all-start = ((bf16[8,1,64,128]{3,2,1,0:T(8,128)(2,1)}), bf16[8,1,64,128]{3,2,1,0:T(8,128)(2,1)S(1)}, u32[]{:S(2)}, u32[]{:S(2)}) async-start(bf16[8,1,64,128]{3,2,1,0:T(8,128)(2,1)} %bitcast.21), calls=%async_computation | async-start | bytes 262144 | tf_op jit(solution)/shard_map/all_to_all | solution.py:99
  28.1 7.3 %all-to-all-done = bf16[8,1,64,128]{3,2,1,0:T(8,128)(2,1)S(1)} async-done(((bf16[8,1,64,128]{3,2,1,0:T(8,128)(2,1)}), bf16[8,1,64,128]{3,2,1,0:T(8,128)(2,1)S(1)}, u32[]{:S(2)}, u32[]{:S(2)}) %all-to-all-start) | async-done | bytes 131104 | tf_op jit(solution)/shard_map/all_to_all | solution.py:99
  35.4 0.1 reshape_reshape.3
  35.5 0.2 convolution_bitcast_fusion
  35.8 0.1 fusion.29
  35.9 11.0 %all-reduce.1 = (f32[64,64]{1,0:T(8,128)S(1)}, f32[64,64]{1,0:T(8,128)S(1)}) all-reduce(f32[64,64]{1,0:T(8,128)S(1)} %get-tuple-element.424, f32[64,64]{1,0:T(8,128)S(1)} %get-tuple-element.423), channel_id=1, replica_groups=mesh['cuts'=8,'batch'=4] {'batch'}, use_global_device_ids=true, to_apply=%region_26.27 | all-reduce | flops 8192 | bytes 65536 | tf_op jit(solution)/shard_map/psum | solution.py:105
  46.9 34.8 %all-reduce = (f32[64,64]{1,0:T(8,128)S(1)}, f32[64,64]{1,0:T(8,128)S(1)}) all-reduce(f32[64,64]{1,0:T(8,128)S(1)} %get-tuple-element.387, f32[64,64]{1,0:T(8,128)S(1)} %get-tuple-element.388), channel_id=1, replica_groups=mesh['cuts'=8,'batch'=4] {'cuts'}, use_global_device_ids=true, to_apply=%region_27.28 | all-reduce | flops 8192 | bytes 65536 | tf_op jit(solution)/shard_map/psum | solution.py:105
  81.7 0.1 fusion.42
  81.8 0.2 fusion.38
  82.0 0.2 convolution_subtract_fusion.1
  82.2 0.1 convolution_add_fusion.1
  82.4 0.2 fusion.36
  82.6 0.2 fusion.34
  82.8 0.2 fusion.25
  83.1 0.1 copy.24
  83.2 0.1 stack_reshape.6
  83.3 0.2 fusion.24
  83.5 0.1 copy.25
  83.6 0.1 stack_reshape.7
  83.7 0.6 copy.26
  84.4 14.1 %gather_fusion.5 = f32[4096,2]{1,0:T(8,128)} fusion(f32[2,4096]{0,1:T(8,128)S(1)} %copy.26, s32[4096]{0:T(1024)S(1)} %fusion.31), kind=kCustom, calls=%fused_computation.5 | custom fusion | bytes 81920 | tf_op jit(solution)/shard_map/gather | solution.py:84
  98.5 0.8 fusion.28
  99.3 0.6 copy.27
  (36 shorter events, 0.3 us)
Async XLA Ops:
  0.0 11.2 %copy-start = (bf16[8,64,128]{2,1,0:T(8,128)(2,1)S(1)}, bf16[8,64,128]{2,1,0:T(8,128)(2,1)}, u32[]{:S(2)}) copy-start(bf16[8,64,128]{2,1,0:T(8,128)(2,1)} %param.25) | copy-start | bytes 393220
  14.9 1.1 %copy-start.5 = (s32[1,8]{1,0:T(1,128)S(1)}, s32[1,8]{1,0:T(1,128)}, u32[]{:S(2)}) copy-start(s32[1,8]{1,0:T(1,128)} %param.30) | copy-start | bytes 100
  14.9 13.1 %copy-start.3 = (s32[4096]{0:T(1024)S(1)}, s32[4096]{0:T(1024)}, u32[]{:S(2)}) copy-start(s32[4096]{0:T(1024)} %param.33) | copy-start | bytes 49156
  14.9 20.6 %copy-start.4 = (bf16[8,64,128]{2,1,0:T(8,128)(2,1)S(1)}, bf16[8,64,128]{2,1,0:T(8,128)(2,1)}, u32[]{:S(2)}) copy-start(bf16[8,64,128]{2,1,0:T(8,128)(2,1)} %param.26) | copy-start | bytes 393220
  15.0 66.7 %copy-start.1 = (bf16[64,128]{1,0:T(8,128)(2,1)S(1)}, bf16[64,128]{1,0:T(8,128)(2,1)}, u32[]{:S(2)}) copy-start(bf16[64,128]{1,0:T(8,128)(2,1)} %param.32) | copy-start | bytes 49156
  15.0 67.4 %copy-start.2 = (bf16[64,128]{1,0:T(8,128)(2,1)S(1)}, bf16[64,128]{1,0:T(8,128)(2,1)}, u32[]{:S(2)}) copy-start(bf16[64,128]{1,0:T(8,128)(2,1)} %param.31) | copy-start | bytes 49156
  17.8 17.6 %all-to-all-start = ((bf16[8,1,64,128]{3,2,1,0:T(8,128)(2,1)}), bf16[8,1,64,128]{3,2,1,0:T(8,128)(2,1)S(1)}, u32[]{:S(2)}, u32[]{:S(2)}) async-start(bf16[8,1,64,128]{3,2,1,0:T(8,128)(2,1)} %bitcast.21), calls=%async_computation | async-start | bytes 262144 | tf_op jit(solution)/shard_map/all_to_all | solution.py:99
